TPU v7x, 32 devices: a whole 2x2x4 slice. The times are simulated.
32 devices in a mesh: ctx: 4 (over z), tp: 4 (over y, core), ep: 2 (over x).
Axes of the slice: x: 2, y: 2, z: 4, core: 2. Of those that a mesh axis runs over, the one named last changes fastest.
Arguments:
- resid: bfloat16 [1024, 6144], P('ctx', ('tp', 'ep')), may hold values from -60 to 60
- queries: bfloat16 [1024, 6144], P('ctx', 'tp'), may hold values from -6 to 6
- keys: bfloat16 [1024, 1024], P('ctx', 'tp'), may hold values from -4 to 4
- values: bfloat16 [1024, 1024], P('ctx', 'tp'), may hold values from -5 to 5
- w_out: bfloat16 [6144, 6144], P('tp', ('ctx', 'ep')), may hold values from -0.078125 to 0.078125
- norm_gain: bfloat16 [6144], P(('tp', 'ep')), may hold values from 0.5 to 1.5
- w_gate: bfloat16 [4, 6144, 8192], P('tp', None, ('ctx', 'ep')), may hold values from -0.078125 to 0.078125
- w_up: bfloat16 [4, 6144, 8192], P('tp', None, ('ctx', 'ep')), may hold values from -0.078125 to 0.078125
- w_down: bfloat16 [4, 8192, 6144], P('tp', ('ctx', 'ep')), may hold values from -0.0625 to 0.0625
- expert_ids: int32 [1024, 2], P('ctx'), may hold values from 0 to 3, all different within a row; in each aligned block of 256 rows (0 to 255, 256 to 511, ...) at most 192 rows name the same one
- route_units: int32 [1024, 2], P('ctx'), may hold values from 1 to 65535
Outputs:
- mixed: bfloat16 [1024, 6144], P('ctx', ('tp', 'ep'))
Inputs may be any that keep to these rules, and one draw needn't show every extreme that they name: `expert_ids`: each row names two different experts; in every aligned block of 256 rows no expert is named by more than 192 rows, a bound that some block reaches.
All inputs are finite; a program needn't handle non-finite values.
Results may differ from a plain program's by a relative error of at most 0.01.
Values may be sent and summed in bfloat16 or wider, within the bound.
A program may use at most 128 MiB of HBM per device.

v0:
```python
import jax
import jax.numpy as jnp
from jax import lax
from jax.sharding import PartitionSpec as P

D = 6144
HD = 128


def from_partner(x, axis, distance):
    return lax.ppermute(x, axis, [(i, i ^ 1 << distance) for i in range(lax.axis_size(axis))])


def on_device(
    resid, queries, keys, values, w_out, norm_gain, w_gate, w_up, w_down, expert_ids, route_units
):
    tp_size = lax.axis_size("tp")
    ep_size = lax.axis_size("ep")
    ctx_size = lax.axis_size("ctx")
    tok_rows = queries.shape[0]
    heads_dev = queries.shape[1] // HD
    kv_dev = keys.shape[1] // HD
    group = heads_dev // kv_dev
    feat_dev = resid.shape[1]
    hidden_dev = w_gate.shape[2]
    capacity = 3 * tok_rows // tp_size
    first_pos = lax.axis_index("ctx") * tok_rows
    query_heads = queries.reshape(tok_rows, kv_dev, group, HD)
    query_pos = first_pos + jnp.arange(tok_rows, dtype=jnp.int32)
    running_max = jnp.full((kv_dev, group, tok_rows), -1e30, jnp.float32)
    key_piece = lax.all_gather(keys, "ctx", axis=0, tiled=True)
    value_piece = lax.all_gather(values, "ctx", axis=0, tiled=True)
    count = key_piece.shape[0]
    key_rows = key_piece.reshape(count, kv_dev, HD)
    value_rows = value_piece.reshape(count, kv_dev, HD)
    scores = jnp.einsum(
        "tkgd,nkd->kgtn", query_heads, key_rows, preferred_element_type=jnp.float32
    ) * HD ** (-0.5)
    key_pos = jnp.arange(count, dtype=jnp.int32)
    allowed = (key_pos[None, :] <= query_pos[:, None])[None, None]
    block_max = jnp.max(jnp.where(allowed, scores, -1e30), axis=-1)
    new_max = jnp.maximum(running_max, block_max)
    probs = jnp.where(allowed, jnp.exp(scores - new_max[..., None]), 0.0)
    new_sum = jnp.sum(probs, axis=-1)
    probs_b = probs.astype(jnp.bfloat16)
    update = jnp.einsum("kgtn,nkd->kgtd", probs_b, value_rows, preferred_element_type=jnp.float32)
    attn = (
        (update / new_sum[..., None])
        .transpose(2, 0, 1, 3)
        .reshape(tok_rows, heads_dev * HD)
        .astype(jnp.bfloat16)
    )
    partial_proj = jnp.dot(
        attn, lax.all_gather(w_out, "ctx", axis=1, tiled=True), preferred_element_type=jnp.float32
    )
    proj = lax.psum_scatter(
        partial_proj.astype(jnp.bfloat16), "tp", scatter_dimension=1, tiled=True
    ).astype(jnp.float32)
    hres = (resid.astype(jnp.float32) + proj).astype(jnp.bfloat16)
    hfloat = hres.astype(jnp.float32)
    square_total = lax.psum(jnp.sum(hfloat * hfloat, axis=1, keepdims=True), ("tp", "ep"))
    normed = (hfloat * lax.rsqrt(square_total / D + 1e-05) * norm_gain.astype(jnp.float32)).astype(
        jnp.bfloat16
    )
    onehot = (expert_ids[..., None] == jnp.arange(tp_size, dtype=jnp.int32)).astype(jnp.int32)
    per_token = jnp.sum(onehot, axis=1)
    earlier = jnp.cumsum(per_token, axis=0) - per_token
    slot = jnp.sum(onehot * earlier[:, None, :], axis=-1)
    codes = expert_ids * capacity + slot
    slot_ids = jnp.arange(tp_size * capacity, dtype=jnp.int32)
    picks = (
        (slot_ids[:, None] == codes[None, :, 0]) | (slot_ids[:, None] == codes[None, :, 1])
    ).astype(jnp.bfloat16)
    dispatched = jnp.dot(picks, normed, preferred_element_type=jnp.float32).astype(jnp.bfloat16)
    dispatched = dispatched.reshape(tp_size, 1, capacity, feat_dev)
    arrived = lax.all_to_all(dispatched, "tp", split_axis=0, concat_axis=1, tiled=True)
    gate_w = w_gate[0].reshape(tp_size, ep_size, feat_dev, hidden_dev)
    up_w = w_up[0].reshape(tp_size, ep_size, feat_dev, hidden_dev)
    zero_acc = jnp.zeros((ctx_size, capacity, hidden_dev), jnp.float32)
    piece = lax.all_gather(arrived, ("ctx", "ep"), axis=0, tiled=True)

    def one_row(index, totals):
        gate_total, up_total = totals
        source = index // ep_size
        parity = index % ep_size
        row = lax.dynamic_index_in_dim(piece, index, 0, keepdims=False)
        gate_part = lax.dynamic_index_in_dim(gate_w, parity, 1, keepdims=False)
        up_part = lax.dynamic_index_in_dim(up_w, parity, 1, keepdims=False)
        gate_add = jnp.einsum("tsj,tjf->sf", row, gate_part, preferred_element_type=jnp.float32)
        up_add = jnp.einsum("tsj,tjf->sf", row, up_part, preferred_element_type=jnp.float32)
        gate_now = lax.dynamic_index_in_dim(gate_total, source, 0, keepdims=False) + gate_add
        up_now = lax.dynamic_index_in_dim(up_total, source, 0, keepdims=False) + up_add
        return (
            lax.dynamic_update_index_in_dim(gate_total, gate_now, source, 0),
            lax.dynamic_update_index_in_dim(up_total, up_now, source, 0),
        )

    gate_acc, up_acc = lax.fori_loop(0, piece.shape[0], one_row, (zero_acc, zero_acc))
    hidden = (jax.nn.silu(gate_acc) * up_acc).astype(jnp.bfloat16)
    down_w = w_down[0].reshape(hidden_dev, tp_size, ep_size, feat_dev)
    parity = lax.axis_index("ep")
    mine_cols = lax.dynamic_index_in_dim(down_w, parity, 2, keepdims=False)
    give_cols = lax.dynamic_index_in_dim(down_w, 1 - parity, 2, keepdims=False)
    got_hidden, got_cols = from_partner((hidden, give_cols), "ep", 0)
    hidden_both = jnp.concatenate([hidden, got_hidden], axis=2)
    cols_both = jnp.concatenate([mine_cols, got_cols], axis=0)
    blocks = lax.axis_size("ctx") * capacity // capacity
    product = jnp.einsum(
        "csf,ftj->cstj", hidden_both, cols_both, preferred_element_type=jnp.float32
    )
    expert_sum = lax.psum_scatter(
        product.reshape(blocks * capacity, tp_size * feat_dev).astype(jnp.bfloat16),
        "ctx",
        scatter_dimension=0,
        tiled=True,
    )
    expert_out = expert_sum.reshape(1, capacity, tp_size, feat_dev)
    returned = lax.all_to_all(expert_out, "tp", split_axis=2, concat_axis=0, tiled=True)
    units = route_units.astype(jnp.float32)
    weights = (units / jnp.sum(units, axis=-1, keepdims=True)).astype(jnp.bfloat16)
    combine = jnp.where(slot_ids[None, :] == codes[:, 0:1], weights[:, 0:1], 0.0) + jnp.where(
        slot_ids[None, :] == codes[:, 1:2], weights[:, 1:2], 0.0
    )
    moe = jnp.dot(
        combine, returned.reshape(tp_size * capacity, feat_dev), preferred_element_type=jnp.float32
    )
    return (hfloat + moe).astype(jnp.bfloat16)


def solution(mesh):
    placed = (
        P("ctx", ("tp", "ep")),
        P("ctx", "tp"),
        P("ctx", "tp"),
        P("ctx", "tp"),
        P("tp", ("ctx", "ep")),
        P(("tp", "ep")),
        P("tp", None, ("ctx", "ep")),
        P("tp", None, ("ctx", "ep")),
        P("tp", ("ctx", "ep"), None),
        P("ctx", None),
        P("ctx", None),
    )
    return jax.shard_map(
        on_device, mesh=mesh, in_specs=placed, out_specs=P("ctx", ("tp", "ep")), check_vma=False
    )
```

profile of v0, /device:TPU:0, one launch (start us, length us, event | category | flops | bytes accessed | tf_op | source)
XLA Modules:
  0.0 699.3 jit_solution(8056801487796941439)
XLA Ops:
  7.3 19.0 %all_gather.13 = bf16[1024,256]{1,0:T(8,128)(2,1)S(1)} all-gather(bf16[256,256]{1,0:T(8,128)(2,1)} %param.16), channel_id=1, replica_groups=mesh['ctx'=4,'tp'=4,'ep'=2] {'ctx'}, dimensions={0}, use_global_device_ids=true | all-gather | bytes 655360 | tf_op jit(solution)/shard_map/all_gather | solution.py:32
  28.9 24.0 %all_gather.12 = bf16[1024,256]{0,1:T(8,128)(2,1)S(1)} all-gather(bf16[256,256]{0,1:T(8,128)(2,1)S(1)} %copy.54), channel_id=1, replica_groups=mesh['ctx'=4,'tp'=4,'ep'=2] {'ctx'}, dimensions={0}, use_global_device_ids=true | all-gather | bytes 655360 | tf_op jit(solution)/shard_map/all_gather | solution.py:31
  60.5 126.2 %all-gather.4.cloned.1.call-done = bf16[1536,3072]{1,0:T(8,128)(2,1)} async-done(((bf16[1536,768]{1,0:T(8,128)(2,1)}), bf16[1536,3072]{1,0:T(8,128)(2,1)}) %all-gather.4.cloned.1.call-update) | async-done | bytes 9437200 | tf_op jit(solution)/shard_map/all_gather | solution.py:54
  186.8 7.5 %convolution_convert_fusion = bf16[256,3072]{1,0:T(8,128)(2,1)} fusion(bf16[256,1536]{0,1:T(8,128)(2,1)S(1)} %bitcast.174, bf16[1536,3072]{1,0:T(8,128)(2,1)} %all-gather.4.cloned.1.call-done), kind=kOutput, calls=%fused_computation.37 | convolution fusion | flops 2416705536 | bytes 11796480 | tf_op jit(solution)/shard_map/dot_general | solution.py:53
  196.1 25.5 %reduce-scatter.3.cloned.1.call-done = bf16[256,768]{1,0:T(8,128)(2,1)} async-done(((bf16[256,3072]{1,0:T(8,128)(2,1)}), bf16[256,768]{1,0:T(8,128)(2,1)}) %reduce-scatter.3.cloned.1.call-update) | async-done | bytes 393232 | tf_op jit(solution)/shard_map/reduce_scatter | solution.py:56
  222.8 13.3 %psum.7 = f32[256,1]{0,1:T(1,128)S(1)} all-reduce(f32[256,1]{0,1:T(1,128)S(1)} %bitcast.180), channel_id=1, replica_groups=mesh['ctx'=4,'tp'=4,'ep'=2] {'tp','ep'}, use_global_device_ids=true, to_apply=%region_9.10 | all-reduce | flops 256 | bytes 2048 | tf_op jit(solution)/shard_map/psum | solution.py:61
  237.7 19.0 %all_to_all.27 = bf16[4,1,192,768]{3,2,1,0:T(8,128)(2,1)} all-to-all(bf16[4,1,192,768]{3,2,1,0:T(8,128)(2,1)S(1)} %bitcast.176), channel_id=1, replica_groups=mesh['ctx'=4,'tp'=4,'ep'=2] {'tp'}, dimensions={0} | all-to-all | bytes 2359296 | tf_op jit(solution)/shard_map/all_to_all | solution.py:76
  257.0 27.5 %reshape_squeeze.11 = bf16[1024,4,2,768]{3,2,1,0:T(2,128)(2,1)} reshape(bf16[1,1024,6144]{2,1,0:T(8,128)(2,1)} %param.21) | data formatting | bytes 25165824 | tf_op jit(solution)/shard_map/reshape;squeeze | solution.py:100
  284.4 29.1 %constant_dynamic-slice_fusion.2 = (bf16[1024,4,1,768]{3,2,1,0:T(2,128)(2,1)}, bf16[1024,4,1,768]{3,2,1,0:T(2,128)(2,1)}) fusion(bf16[1024,4,2,768]{3,2,1,0:T(2,128)(2,1)} %reshape_squeeze.11, s32[]{:T(128)S(6)} %select_n.93, s32[]{:T(128)S(6)} %select_n.94), kind=kLoop, calls=%fused_computation.87 | loop fusion | bytes 25165832 | tf_op jit(solution)/shard_map/jit(dynamic_index_in_dim)/dynamic_slice | solution.py:102
  313.5 9.5 %copy.85 = bf16[1024,4,1,768]{3,0,1,2:T(8,128)(2,1)} copy(bf16[1024,4,1,768]{3,2,1,0:T(2,128)(2,1)} %get-tuple-element.200) | data formatting | bytes 12582912
  324.1 106.9 %all-gather.6.cloned.1.call-done = bf16[32,1,192,768]{3,2,1,0:T(8,128)(2,1)} async-done(((bf16[4,1,192,768]{3,2,1,0:T(8,128)(2,1)}), bf16[32,1,192,768]{3,2,1,0:T(8,128)(2,1)}) %all-gather.6.cloned.1.call-update) | async-done | bytes 9437200 | tf_op jit(solution)/shard_map/all_gather | solution.py:80
  433.5 90.3 %while.17 = (s32[]{:T(128)}, f32[4,192,1024]{2,1,0:T(8,128)S(1)}, f32[4,192,1024]{2,1,0:T(8,128)}, bf16[8,4,192,768]{3,2,1,0:T(8,128)(2,1)}, bf16[4,2,768,1024]{...) while((s32[]{:T(128)}, f32[4,192,1024]{2,1,0:T(8,128)S(1)}, ...), condition=%wide.region_11.12_spmd, body=%wide.region_10.11_spmd.sunk | while | flops 2416312320 | bytes 21233992 | solution.py:98
  434.8 4.6 fusion.97
  439.3 5.5 fusion.98
  446.1 4.6 fusion.97
  450.7 5.5 fusion.98
  457.4 4.6 fusion.97
  462.0 5.4 fusion.98
  468.7 4.6 fusion.97
  473.2 5.4 fusion.98
  480.0 4.6 fusion.97
  484.5 5.4 fusion.98
  491.2 4.6 fusion.97
  495.8 5.4 fusion.98
  507.1 5.5 fusion.98
  513.8 4.6 fusion.97
  518.3 5.5 fusion.98
  527.8 6.7 copy.86
  534.6 28.3 %collective-permute-done = bf16[4,192,1024]{2,1,0:T(8,128)(2,1)} collective-permute-done((bf16[4,192,1024]{2,1,0:T(8,128)(2,1)}, bf16[4,192,1024]{2,1,0:T(8,128)(2,1)}, u32[]{:S(2)}, u32[]{:S(2)}) %collective-permute-start) | collective-permute-done | bytes 1572896 | tf_op jit(solution)/shard_map/ppermute | solution.py:11
  562.8 13.0 %fusion.49 = bf16[4,192,4,768]{3,1,2,0:T(8,128)(2,1)S(1)} fusion(bf16[1024,4,768]{2,0,1:T(8,128)(2,1)} %collective-permute-done.1, bf16[1024,4,768]{2,0,1:T(8,128)(2,1)S(1)} %bitcast.171, bf16[4,192,1024]{2,1,0:T(8,128)(2,1)} %collective-permute-done, bf16[4,192,1024]{2,1,0:T(8,128)(2,1)} %multiply_convert_fusion), kind=kOutput, calls=%fused_computation.42 | convolution fusion | flops 9697492992 | bytes 20447232 | tf_op jit(solution)/shard_map/csf,ftj->cstj/dot_general | solution.py:108
  582.7 85.5 %reduce-scatter.5.cloned.1.call-done = bf16[192,3072]{1,0:T(8,128)(2,1)} async-done(((bf16[768,3072]{1,0:T(8,128)(2,1)}), bf16[192,3072]{1,0:T(8,128)(2,1)}) %reduce-scatter.5.cloned.1.call-update) | async-done | bytes 1179664 | tf_op jit(solution)/shard_map/reduce_scatter | solution.py:111
  675.6 15.7 %all-to-all-done.1 = bf16[1,192,4,768]{3,1,0,2:T(8,128)(2,1)S(1)} async-done(((bf16[1,192,4,768]{3,1,0,2:T(8,128)(2,1)}), bf16[1,192,4,768]{3,1,0,2:T(8,128)(2,1)S(1)}, u32[]{:S(2)}, u32[]{:S(2)}) %all-to-all-start.1) | async-done | bytes 1179680 | tf_op jit(solution)/shard_map/all_to_all | solution.py:118
  (68 shorter events, 53.6 us)
Async XLA Ops:
  6.5 180.2 %all-gather.4.cloned.1.call-start = ((), (), s32[]{:S(2)}) async-start(), calls=%async_computation.4 | async-start | bytes 11796480 | tf_op jit(solution)/shard_map/all_gather | solution.py:54
  7.3 214.3 %reduce-scatter.3.cloned.1.call-start = ((), (), s32[]{:S(2)}) async-start(), calls=%async_computation.5 | async-start | bytes 1966080 | tf_op jit(solution)/shard_map/reduce_scatter | solution.py:56
  186.8 7.6 %copy-start.4 = (bf16[768]{0:T(1024)(128)(2,1)S(1)}, bf16[768]{0:T(1024)(128)(2,1)}, u32[]{:S(2)}) copy-start(bf16[768]{0:T(1024)(128)(2,1)} %param.18) | copy-start | bytes 4612
  186.8 7.6 %copy-start.2 = (s32[256,2]{0,1:T(2,128)S(1)}, s32[256,2]{0,1:T(2,128)}, u32[]{:S(2)}) copy-start(s32[256,2]{0,1:T(2,128)} %param.22) | copy-start | bytes 6148
  186.8 34.8 %copy-start = (bf16[256,768]{1,0:T(8,128)(2,1)S(1)}, bf16[256,768]{1,0:T(8,128)(2,1)}, u32[]{:S(2)}) copy-start(bf16[256,768]{1,0:T(8,128)(2,1)} %param.13) | copy-start | bytes 1179652
  194.3 236.7 %all-gather.6.cloned.1.call-start = ((), (), s32[]{:S(2)}) async-start(), calls=%async_computation.7 | async-start | bytes 10616832 | tf_op jit(solution)/shard_map/all_gather | solution.py:80
  256.8 411.4 %reduce-scatter.5.cloned.1.call-start = ((), (), s32[]{:S(2)}) async-start(), calls=%async_computation.6 | async-start | bytes 5898240 | tf_op jit(solution)/shard_map/reduce_scatter | solution.py:111
  323.1 211.5 %collective-permute-start.1 = (bf16[1024,4,768]{2,0,1:T(8,128)(2,1)}, bf16[1024,4,768]{2,0,1:T(8,128)(2,1)}, u32[]{:S(2)}, u32[]{:S(2)}) collective-permute-start(bf16[1024,4,768]{2,0,1:T(8,128)(2,1)} %bitcast.144), channel_id=1, source_target_pairs={{0,1},{1,0},{2,3},{3,2},{4,5},{5,4},{6,7},{7,6},{8,9},{9,8},{10,11... | collective-permute-start | bytes 18874376 | tf_op jit(solution)/shard_map/ppermute | solution.py:11
  527.8 35.0 %collective-permute-start = (bf16[4,192,1024]{2,1,0:T(8,128)(2,1)}, bf16[4,192,1024]{2,1,0:T(8,128)(2,1)}, u32[]{:S(2)}, u32[]{:S(2)}) collective-permute-start(bf16[4,192,1024]{2,1,0:T(8,128)(2,1)} %multiply_convert_fusion), channel_id=1, source_target_pairs={{0,1},{1,0},{2,3},{3,2},{4,5},{5,4},{6,7},{7,6},{8,9},{9,8},{10,11... | collective-permute-start | bytes 4718600 | tf_op jit(solution)/shard_map/ppermute | solution.py:11
  582.7 92.9 %copy-start.3 = (s32[256,2]{0,1:T(2,128)S(1)}, s32[256,2]{0,1:T(2,128)}, u32[]{:S(2)}) copy-start(s32[256,2]{0,1:T(2,128)} %param.23) | copy-start | bytes 6148
  582.7 108.7 %copy-start.1 = (bf16[256,768]{1,0:T(8,128)(2,1)S(1)}, bf16[256,768]{1,0:T(8,128)(2,1)}, u32[]{:S(2)}) copy-start(bf16[256,768]{1,0:T(8,128)(2,1)} %reduce-scatter.3.cloned.1.call-done) | copy-start | bytes 1179652
  672.0 19.3 %all-to-all-start.1 = ((bf16[1,192,4,768]{3,1,0,2:T(8,128)(2,1)}), bf16[1,192,4,768]{3,1,0,2:T(8,128)(2,1)S(1)}, u32[]{:S(2)}, u32[]{:S(2)}) async-start(bf16[1,192,4,768]{3,1,0,2:T(8,128)(2,1)} %copy.68), calls=%async_computation.3 | async-start | bytes 2359296 | tf_op jit(solution)/shard_map/all_to_all | solution.py:118
Sparse Core Ops, SparseCore 0:
  8.9 177.8 all-gather.3
  194.4 27.0 reduce-scatter.2
  256.9 174.1 all-gather.5
  582.8 85.2 reduce-scatter.4
where the time goes:
time: 701 us; the launch traced here: 699 us
  waiting for transfers between devices  389 us (55%)
  matrix products  108 us (15%)
  local copies, waits for them, and re-layouts  98.9 us (14%)
  blocking collectives  75.3 us (11%)
  between operations  13.3 us (2%)
  other arithmetic  9.34 us (1%)
    all_gather x1, waiting for transfers between devices, on_device(): lax.all_gather(w_out, 'ctx', axis=1, tiled=True)  126 us
    all_gather x1, waiting for transfers between devices, on_device(): piece = lax.all_gather(arrived, ('ctx', 'ep'), axis=0, tiled=True)  107 us
    reduce_scatter x1, waiting for transfers between devices, on_device(): lax.psum_scatter(product.reshape(blocks * capacity, tp_size * feat_dev).a...  85.5 us
    dot_general x8, matrix products, one_row(): jnp.einsum('tsj,tjf->sf', row, up_part, preferred_element_type=jnp.float32)  43.6 us
    dot_general x8, matrix products, one_row(): jnp.einsum('tsj,tjf->sf', row, gate_part, preferred_element_type=jnp.floa...  36.5 us
    dynamic_slice x1, local copies, waits for them, and re-layouts, on_device(): mine_cols = lax.dynamic_index_in_dim(down_w, parity, 2, keepdims=False)  29.1 us
    ppermute x2, waiting for transfers between devices, from_partner(): lax.ppermute(x, axis, [(i, i ^ 1 << distance) for i in range(lax.axis_siz...  28.3 us
    another operation x1, local copies, waits for them, and re-layouts, on_device(): down_w = w_down[0].reshape(hidden_dev, tp_size, ep_size, feat_dev)  27.5 us
  transfers between devices with their start and end apart: 7, of which 6 were waited for; matrix products, arithmetic and copies ran while one was open for 26% of the time, Pallas kernels for 0%

commit v1 on v0

--- a/solution.py
+++ b/solution.py
@@ -77,7 +77,10 @@
     gate_w = w_gate[0].reshape(tp_size, ep_size, feat_dev, hidden_dev)
     up_w = w_up[0].reshape(tp_size, ep_size, feat_dev, hidden_dev)
     zero_acc = jnp.zeros((ctx_size, capacity, hidden_dev), jnp.float32)
-    piece = lax.all_gather(arrived, ("ctx", "ep"), axis=0, tiled=True)
+    piece = jnp.concatenate(
+        lax.all_to_all(jnp.stack([arrived] * lax.axis_size(("ctx", "ep"))), ("ctx", "ep"), 0, 0),
+        axis=0,
+    )
 
     def one_row(index, totals):
         gate_total, up_total = totals

time: 701 us -> 741 us (1.057)
  waiting for transfers between devices: 389 us -> 418 us
    all_to_all x0 -> x1, waiting for transfers between devices: none -> 138 us  [on_device(): lax.all_to_all(jnp.stack([arrived] * lax.axis_size(('ctx', 'ep'))), ('ctx...]
    all_gather x1 -> x0, waiting for transfers between devices: 107 us -> none  [on_device(): piece = lax.all_gather(arrived, ('ctx', 'ep'), axis=0, tiled=True)]
  transfers between devices with their start and end apart: 7 -> 7, of which waited for: 6 -> 6; matrix products, arithmetic and copies ran while one was open for 26% -> 24% of each run, Pallas kernels for 0% -> 0%
where the time goes in v1:
time: 741 us; the launch traced here: 739 us
  waiting for transfers between devices  418 us (56%)
  matrix products  108 us (15%)
  local copies, waits for them, and re-layouts  103 us (14%)
  blocking collectives  74.6 us (10%)
  between operations  13.3 us (2%)
  starting transfers between devices  12 us (2%)
  other arithmetic  9.34 us (1%)
    all_to_all x1, waiting for transfers between devices, on_device(): lax.all_to_all(jnp.stack([arrived] * lax.axis_size(('ctx', 'ep'))), ('ctx...  138 us
    all_gather x1, waiting for transfers between devices, on_device(): lax.all_gather(w_out, 'ctx', axis=1, tiled=True)  126 us
    reduce_scatter x1, waiting for transfers between devices, on_device(): lax.psum_scatter(product.reshape(blocks * capacity, tp_size * feat_dev).a...  85 us
    dot_general x8, matrix products, one_row(): jnp.einsum('tsj,tjf->sf', row, up_part, preferred_element_type=jnp.float32)  43.6 us
    dot_general x8, matrix products, one_row(): jnp.einsum('tsj,tjf->sf', row, gate_part, preferred_element_type=jnp.floa...  36.5 us
    dynamic_slice x1, local copies, waits for them, and re-layouts, on_device(): mine_cols = lax.dynamic_index_in_dim(down_w, parity, 2, keepdims=False)  29.1 us
    another operation x1, local copies, waits for them, and re-layouts, on_device(): down_w = w_down[0].reshape(hidden_dev, tp_size, ep_size, feat_dev)  27.4 us
    ppermute x2, waiting for transfers between devices, from_partner(): lax.ppermute(x, axis, [(i, i ^ 1 << distance) for i in range(lax.axis_siz...  27.3 us
  transfers between devices with their start and end apart: 7, of which 6 were waited for; matrix products, arithmetic and copies ran while one was open for 24% of the time, Pallas kernels for 0%

profile of v1, /device:TPU:0, one launch (start us, length us, event | category | flops | bytes accessed | tf_op | source)
XLA Modules:
  0.0 739.3 jit_solution(14117879943570221539)
XLA Ops:
  7.3 19.0 %all_gather.10 = bf16[1024,256]{1,0:T(8,128)(2,1)S(1)} all-gather(bf16[256,256]{1,0:T(8,128)(2,1)} %param.16), channel_id=1, replica_groups=mesh['ctx'=4,'tp'=4,'ep'=2] {'ctx'}, dimensions={0}, use_global_device_ids=true | all-gather | bytes 655360 | tf_op jit(solution)/shard_map/all_gather | solution.py:32
  28.9 24.0 %all_gather.9 = bf16[1024,256]{0,1:T(8,128)(2,1)S(1)} all-gather(bf16[256,256]{0,1:T(8,128)(2,1)S(1)} %copy.54), channel_id=1, replica_groups=mesh['ctx'=4,'tp'=4,'ep'=2] {'ctx'}, dimensions={0}, use_global_device_ids=true | all-gather | bytes 655360 | tf_op jit(solution)/shard_map/all_gather | solution.py:31
  60.5 126.2 %all-gather.2.cloned.1.call-done = bf16[1536,3072]{1,0:T(8,128)(2,1)} async-done(((bf16[1536,768]{1,0:T(8,128)(2,1)}), bf16[1536,3072]{1,0:T(8,128)(2,1)}) %all-gather.2.cloned.1.call-update) | async-done | bytes 9437200 | tf_op jit(solution)/shard_map/all_gather | solution.py:54
  186.8 7.5 %convolution_convert_fusion = bf16[256,3072]{1,0:T(8,128)(2,1)} fusion(bf16[256,1536]{0,1:T(8,128)(2,1)S(1)} %bitcast.175, bf16[1536,3072]{1,0:T(8,128)(2,1)} %all-gather.2.cloned.1.call-done), kind=kOutput, calls=%fused_computation.37 | convolution fusion | flops 2416705536 | bytes 11796480 | tf_op jit(solution)/shard_map/dot_general | solution.py:53
  196.0 25.5 %reduce-scatter.3.cloned.1.call-done = bf16[256,768]{1,0:T(8,128)(2,1)} async-done(((bf16[256,3072]{1,0:T(8,128)(2,1)}), bf16[256,768]{1,0:T(8,128)(2,1)}) %reduce-scatter.3.cloned.1.call-update) | async-done | bytes 393232 | tf_op jit(solution)/shard_map/reduce_scatter | solution.py:56
  222.8 13.3 %psum.7 = f32[256,1]{0,1:T(1,128)S(1)} all-reduce(f32[256,1]{0,1:T(1,128)S(1)} %bitcast.181), channel_id=1, replica_groups=mesh['ctx'=4,'tp'=4,'ep'=2] {'tp','ep'}, use_global_device_ids=true, to_apply=%region_9.10 | all-reduce | flops 256 | bytes 2048 | tf_op jit(solution)/shard_map/psum | solution.py:61
  237.7 18.3 %all_to_all.29 = bf16[4,1,192,768]{3,2,1,0:T(8,128)(2,1)S(1)} all-to-all(bf16[4,1,192,768]{3,2,1,0:T(8,128)(2,1)S(1)} %bitcast.177), channel_id=1, replica_groups=mesh['ctx'=4,'tp'=4,'ep'=2] {'tp'}, dimensions={0} | all-to-all | bytes 2359296 | tf_op jit(solution)/shard_map/all_to_all | solution.py:76
  256.0 4.6 stack.5
  260.6 5.0 all-to-all-start.1
  265.9 27.4 %reshape_squeeze.11 = bf16[1024,4,2,768]{3,2,1,0:T(2,128)(2,1)} reshape(bf16[1,1024,6144]{2,1,0:T(8,128)(2,1)} %param.21) | data formatting | bytes 25165824 | tf_op jit(solution)/shard_map/reshape;squeeze | solution.py:103
  293.2 29.1 %constant_dynamic-slice_fusion.2 = (bf16[1024,4,1,768]{3,2,1,0:T(2,128)(2,1)}, bf16[1024,4,1,768]{3,2,1,0:T(2,128)(2,1)}) fusion(bf16[1024,4,2,768]{3,2,1,0:T(2,128)(2,1)} %reshape_squeeze.11, s32[]{:T(128)S(6)} %select_n.93, s32[]{:T(128)S(6)} %select_n.94), kind=kLoop, calls=%fused_computation.87 | loop fusion | bytes 25165832 | tf_op jit(solution)/shard_map/jit(dynamic_index_in_dim)/dynamic_slice | solution.py:105
  322.3 9.4 %copy.85 = bf16[1024,4,1,768]{3,0,1,2:T(8,128)(2,1)} copy(bf16[1024,4,1,768]{3,2,1,0:T(2,128)(2,1)} %get-tuple-element.200) | data formatting | bytes 12582912
  333.4 137.7 %all-to-all-done.1 = bf16[8,1,4,192,768]{4,3,2,1,0:T(8,128)(2,1)} async-done(((bf16[8,1,4,192,768]{4,3,2,1,0:T(8,128)(2,1)}), bf16[8,1,4,192,768]{4,3,2,1,0:T(8,128)(2,1)}, u32[]{:S(2)}, u32[]{:S(2)}) %all-to-all-start.1) | async-done | bytes 9437216 | tf_op jit(solution)/shard_map/all_to_all | solution.py:81
  473.6 90.3 %while.17 = (s32[]{:T(128)}, f32[4,192,1024]{2,1,0:T(8,128)S(1)}, f32[4,192,1024]{2,1,0:T(8,128)}, bf16[8,4,192,768]{3,2,1,0:T(8,128)(2,1)}, bf16[4,2,768,1024]{...) while((s32[]{:T(128)}, f32[4,192,1024]{2,1,0:T(8,128)S(1)}, ...), condition=%wide.region_11.12_spmd, body=%wide.region_10.11_spmd.sunk | while | flops 2416312320 | bytes 21233992 | solution.py:101
  474.9 4.6 fusion.97
  479.4 5.5 fusion.98
  486.2 4.6 fusion.97
  490.7 5.5 fusion.98
  502.1 5.4 fusion.98
  508.8 4.6 fusion.97
  513.3 5.4 fusion.98
  520.0 4.6 fusion.97
  524.6 5.4 fusion.98
  535.9 5.4 fusion.98
  547.1 5.5 fusion.98
  553.9 4.6 fusion.97
  558.4 5.5 fusion.98
  569.4 6.7 copy.86
  576.1 27.3 %collective-permute-done = bf16[4,192,1024]{2,1,0:T(8,128)(2,1)} collective-permute-done((bf16[4,192,1024]{2,1,0:T(8,128)(2,1)}, bf16[4,192,1024]{2,1,0:T(8,128)(2,1)}, u32[]{:S(2)}, u32[]{:S(2)}) %collective-permute-start) | collective-permute-done | bytes 1572896 | tf_op jit(solution)/shard_map/ppermute | solution.py:11
  603.3 13.0 %fusion.49 = bf16[4,192,4,768]{3,1,2,0:T(8,128)(2,1)S(1)} fusion(bf16[1024,4,768]{2,0,1:T(8,128)(2,1)} %collective-permute-done.1, bf16[1024,4,768]{2,0,1:T(8,128)(2,1)S(1)} %bitcast.171, bf16[4,192,1024]{2,1,0:T(8,128)(2,1)} %collective-permute-done, bf16[4,192,1024]{2,1,0:T(8,128)(2,1)} %multiply_convert_fusion), kind=kOutput, calls=%fused_computation.42 | convolution fusion | flops 9697492992 | bytes 20447232 | tf_op jit(solution)/shard_map/csf,ftj->cstj/dot_general | solution.py:111
  623.2 85.0 %reduce-scatter.5.cloned.1.call-done = bf16[192,3072]{1,0:T(8,128)(2,1)} async-done(((bf16[768,3072]{1,0:T(8,128)(2,1)}), bf16[192,3072]{1,0:T(8,128)(2,1)}) %reduce-scatter.5.cloned.1.call-update) | async-done | bytes 1179664 | tf_op jit(solution)/shard_map/reduce_scatter | solution.py:114
  715.7 15.7 %all-to-all-done.2 = bf16[1,192,4,768]{3,1,0,2:T(8,128)(2,1)S(1)} async-done(((bf16[1,192,4,768]{3,1,0,2:T(8,128)(2,1)}), bf16[1,192,4,768]{3,1,0,2:T(8,128)(2,1)S(1)}, u32[]{:S(2)}, u32[]{:S(2)}) %all-to-all-start.2) | async-done | bytes 1179680 | tf_op jit(solution)/shard_map/all_to_all | solution.py:121
  (68 shorter events, 64.7 us)
Async XLA Ops:
  6.5 180.2 %all-gather.2.cloned.1.call-start = ((), (), s32[]{:S(2)}) async-start(), calls=%async_computation.5 | async-start | bytes 11796480 | tf_op jit(solution)/shard_map/all_gather | solution.py:54
  7.3 214.3 %reduce-scatter.3.cloned.1.call-start = ((), (), s32[]{:S(2)}) async-start(), calls=%async_computation.6 | async-start | bytes 1966080 | tf_op jit(solution)/shard_map/reduce_scatter | solution.py:56
  186.8 7.6 %copy-start.4 = (bf16[768]{0:T(1024)(128)(2,1)S(1)}, bf16[768]{0:T(1024)(128)(2,1)}, u32[]{:S(2)}) copy-start(bf16[768]{0:T(1024)(128)(2,1)} %param.18) | copy-start | bytes 4612
  186.8 7.6 %copy-start.2 = (s32[256,2]{0,1:T(2,128)S(1)}, s32[256,2]{0,1:T(2,128)}, u32[]{:S(2)}) copy-start(s32[256,2]{0,1:T(2,128)} %param.22) | copy-start | bytes 6148
  186.8 34.8 %copy-start = (bf16[256,768]{1,0:T(8,128)(2,1)S(1)}, bf16[256,768]{1,0:T(8,128)(2,1)}, u32[]{:S(2)}) copy-start(bf16[256,768]{1,0:T(8,128)(2,1)} %param.13) | copy-start | bytes 1179652
  260.6 210.5 %all-to-all-start.1 = ((bf16[8,1,4,192,768]{4,3,2,1,0:T(8,128)(2,1)}), bf16[8,1,4,192,768]{4,3,2,1,0:T(8,128)(2,1)}, u32[]{:S(2)}, u32[]{:S(2)}) async-start(bf16[8,1,4,192,768]{4,3,2,1,0:T(8,128)(2,1)} %stack.5), calls=%async_computation.2 | async-start | bytes 18874368 | tf_op jit(solution)/shard_map/all_to_all | solution.py:81
  265.6 442.6 %reduce-scatter.5.cloned.1.call-start = ((), (), s32[]{:S(2)}) async-start(), calls=%async_computation.7 | async-start | bytes 5898240 | tf_op jit(solution)/shard_map/reduce_scatter | solution.py:114
  331.7 244.3 %collective-permute-start.1 = (bf16[1024,4,768]{2,0,1:T(8,128)(2,1)}, bf16[1024,4,768]{2,0,1:T(8,128)(2,1)}, u32[]{:S(2)}, u32[]{:S(2)}) collective-permute-start(bf16[1024,4,768]{2,0,1:T(8,128)(2,1)} %bitcast.145), channel_id=1, source_target_pairs={{0,1},{1,0},{2,3},{3,2},{4,5},{5,4},{6,7},{7,6},{8,9},{9,8},{10,11... | collective-permute-start | bytes 18874376 | tf_op jit(solution)/shard_map/ppermute | solution.py:11
  567.9 35.4 %collective-permute-start = (bf16[4,192,1024]{2,1,0:T(8,128)(2,1)}, bf16[4,192,1024]{2,1,0:T(8,128)(2,1)}, u32[]{:S(2)}, u32[]{:S(2)}) collective-permute-start(bf16[4,192,1024]{2,1,0:T(8,128)(2,1)} %multiply_convert_fusion), channel_id=1, source_target_pairs={{0,1},{1,0},{2,3},{3,2},{4,5},{5,4},{6,7},{7,6},{8,9},{9,8},{10,11... | collective-permute-start | bytes 4718600 | tf_op jit(solution)/shard_map/ppermute | solution.py:11
  623.2 92.4 %copy-start.3 = (s32[256,2]{0,1:T(2,128)S(1)}, s32[256,2]{0,1:T(2,128)}, u32[]{:S(2)}) copy-start(s32[256,2]{0,1:T(2,128)} %param.23) | copy-start | bytes 6148
  623.2 108.2 %copy-start.1 = (bf16[256,768]{1,0:T(8,128)(2,1)S(1)}, bf16[256,768]{1,0:T(8,128)(2,1)}, u32[]{:S(2)}) copy-start(bf16[256,768]{1,0:T(8,128)(2,1)} %reduce-scatter.3.cloned.1.call-done) | copy-start | bytes 1179652
  712.1 19.3 %all-to-all-start.2 = ((bf16[1,192,4,768]{3,1,0,2:T(8,128)(2,1)}), bf16[1,192,4,768]{3,1,0,2:T(8,128)(2,1)S(1)}, u32[]{:S(2)}, u32[]{:S(2)}) async-start(bf16[1,192,4,768]{3,1,0,2:T(8,128)(2,1)} %copy.68), calls=%async_computation.4 | async-start | bytes 2359296 | tf_op jit(solution)/shard_map/all_to_all | solution.py:121
Sparse Core Ops, SparseCore 0:
  8.9 177.8 all-gather.1
  194.4 27.0 reduce-scatter.2
  623.4 84.8 reduce-scatter.4
